TPU v7x, 32 devices: a whole 2x2x4 slice. The times are simulated.
32 devices in a mesh: dp: 8 (over z, x), expert: 4 (over y, core).
Axes of the slice: x: 2, y: 2, z: 4, core: 2. Of those that a mesh axis runs over, the one named last changes fastest.
Arguments:
- tokens: bfloat16 [4096, 2048], P(('dp', 'expert')), may hold values from -6 to 6
- cotangent: bfloat16 [4096, 2048], P(('dp', 'expert')), may hold values from -6 to 6
- expert_ids: int32 [4096, 2], P(('dp', 'expert')), may hold values from 0 to 3, all different within a row; in each aligned block of 128 rows (0 to 127, 128 to 255, ...) at most 72 rows name the same one
- route_share: float32 [4096], P(('dp', 'expert')), may hold values from 0.5 to 0.95
- gate_proj: bfloat16 [4, 7168, 2048], P('expert', 'dp'), may hold values from -0.125 to 0.125
- up_proj: bfloat16 [4, 7168, 2048], P('expert', 'dp'), may hold values from -0.125 to 0.125
- down_anchor: float32 [4, 7168, 2048], P('expert', 'dp'), may hold values from -0.12 to 0.12
- down_average: float32 [4, 7168, 2048], P('expert', 'dp'), may hold values from -0.12 to 0.12
- down_moment: float32 [4, 7168, 2048], P('expert', 'dp'), may hold values from 0.002 to 0.05
Outputs:
- new_anchor: float32 [4, 7168, 2048], P('expert', 'dp')
- new_average: float32 [4, 7168, 2048], P('expert', 'dp')
- new_moment: float32 [4, 7168, 2048], P('expert', 'dp')
Inputs may be any that keep to these rules, and one draw needn't show every extreme that they name: `expert_ids`: the two ids of a token differ. The rows of one device name any expert at most 72 times, and in every draw some device names some expert exactly 72 times.
All inputs are finite; a program needn't handle non-finite values.
Results may differ from a plain program's by a relative error of at most 0.0043.
Values may be sent and summed in bfloat16 or wider, within the bound.
A program may use at most 192 MiB of HBM per device.

v0:
```python
import jax
import jax.numpy as jnp
from jax import lax
from jax.sharding import PartitionSpec as P

FF = 7168
TOPK = 2
beta_one = 0.9
beta_two = 0.95
learn_rate = 0.05
decay_rate = 0.1
step_count = 4.0
epsilon = 1e-08


def expert_terms(pieces, weight_gate, weight_up):
    rows_in, gated_rows = pieces
    gate_act = lax.dot_general(
        rows_in, weight_gate, (((1,), (1,)), ((), ())), preferred_element_type=jnp.float32
    )
    up_act = lax.dot_general(
        rows_in, weight_up, (((1,), (1,)), ((), ())), preferred_element_type=jnp.float32
    )
    hidden = (jax.nn.silu(gate_act) * up_act).astype(jnp.bfloat16)
    return lax.dot_general(
        hidden, gated_rows, (((0,), (0,)), ((), ())), preferred_element_type=jnp.float32
    )


def routed_shards(
    tokens,
    cotangent,
    expert_ids,
    route_share,
    gate_proj,
    up_proj,
    down_anchor,
    down_average,
    down_moment,
):
    experts_all = lax.axis_size("expert")
    tok_rows = tokens.shape[0]
    width = tokens.shape[1]
    capacity = tok_rows * TOPK // experts_all * 9 // 8
    slots = experts_all * capacity
    shares = jnp.stack([route_share, 1.0 - route_share], axis=1)
    expert_range = jnp.arange(experts_all, dtype=jnp.int32)
    flat_ids = expert_ids.reshape(-1)
    onehot_routes = (flat_ids[:, None] == expert_range[None, :]).astype(jnp.int32)
    earlier = jnp.cumsum(onehot_routes, axis=0) - onehot_routes
    slot_of = jnp.sum(earlier * onehot_routes, axis=1)
    target = (flat_ids * capacity + slot_of).reshape(tok_rows, TOPK)
    slot_range = jnp.arange(slots, dtype=jnp.int32)
    placed = target[None, :, :] == slot_range[:, None, None]
    picker = jnp.sum(placed.astype(jnp.float32), axis=2).astype(jnp.bfloat16)
    slot_share = jnp.sum(jnp.where(placed, shares[None, :, :], 0.0), axis=(1, 2))
    send_rows = jnp.dot(picker, tokens, preferred_element_type=jnp.float32).astype(jnp.bfloat16)
    send_grad = (
        slot_share[:, None] * jnp.dot(picker, cotangent, preferred_element_type=jnp.float32)
    ).astype(jnp.bfloat16)
    weight_gate = gate_proj[0]
    weight_up = up_proj[0]
    arrived = (
        lax.all_to_all(
            send_rows.reshape(experts_all, capacity, width),
            "expert",
            split_axis=0,
            concat_axis=0,
            tiled=True,
        ),
        lax.all_to_all(
            send_grad.reshape(experts_all, capacity, width),
            "expert",
            split_axis=0,
            concat_axis=0,
            tiled=True,
        ),
    )
    rows_here = arrived[0].reshape(slots, width)
    grad_here = arrived[1].reshape(slots, width)
    gradient = expert_terms(
        (
            lax.all_gather(rows_here, "dp", axis=0, tiled=True),
            lax.all_gather(grad_here, "dp", axis=0, tiled=True),
        ),
        weight_gate,
        weight_up,
    )
    gradient = gradient[None] * FF ** (-0.5)
    bias_two = 1.0 - beta_two**step_count
    eval_point = (1.0 - beta_one) * down_anchor + beta_one * down_average
    second_moment = beta_two * down_moment + (1.0 - beta_two) * gradient * gradient
    update_dir = gradient / (jnp.sqrt(second_moment / bias_two) + epsilon) + decay_rate * eval_point
    new_anchor = down_anchor - learn_rate * update_dir
    new_average = (1.0 - 1.0 / step_count) * down_average + 1.0 / step_count * new_anchor
    return (new_anchor, new_average, second_moment)


def adam(gradient, down_anchor, down_average, down_moment):
    bias_two = 1.0 - beta_two**step_count
    eval_point = (1.0 - beta_one) * down_anchor + beta_one * down_average
    second_moment = beta_two * down_moment + (1.0 - beta_two) * gradient * gradient
    update_dir = gradient / (jnp.sqrt(second_moment / bias_two) + epsilon) + decay_rate * eval_point
    new_anchor = down_anchor - learn_rate * update_dir
    new_average = (1.0 - 1.0 / step_count) * down_average + 1.0 / step_count * new_anchor
    return (new_anchor, new_average, second_moment)


def expert_shares(expert_ids, route_share, experts):
    shares = jnp.stack([route_share, 1.0 - route_share], axis=0)
    expert_range = jnp.arange(experts, dtype=jnp.int32)
    named = expert_ids.T[:, None, :] == expert_range[None, :, None]
    return jnp.sum(jnp.where(named, shares[:, None, :], 0.0), axis=0)


def dense_shards(
    tokens,
    cotangent,
    expert_ids,
    route_share,
    gate_proj,
    up_proj,
    down_anchor,
    down_average,
    down_moment,
):
    experts_all = lax.axis_size("expert")
    axes = ("dp", "expert")
    table = expert_shares(expert_ids, route_share, experts_all)
    share = lax.all_gather(table, axes, axis=1, tiled=True)
    share = lax.dynamic_index_in_dim(share, lax.axis_index("expert"), 0, keepdims=True)
    rows = lax.all_gather(tokens, axes, axis=0, tiled=True)
    grads = lax.all_gather(cotangent, axes, axis=0, tiled=True)
    dims = (((1,), (1,)), ((), ()))
    gate_act = lax.dot_general(gate_proj[0], rows, dims, preferred_element_type=jnp.float32)
    up_act = lax.dot_general(up_proj[0], rows, dims, preferred_element_type=jnp.float32)
    hidden = (jax.nn.silu(gate_act) * up_act * share).astype(jnp.bfloat16)
    gradient = jnp.dot(hidden, grads, preferred_element_type=jnp.float32)
    return adam(gradient[None] * FF ** (-0.5), down_anchor, down_average, down_moment)


def solution(mesh):
    placed = (
        P(("dp", "expert"), None),
        P(("dp", "expert"), None),
        P(("dp", "expert"), None),
        P(("dp", "expert")),
        P("expert", "dp", None),
        P("expert", "dp", None),
        P("expert", "dp", None),
        P("expert", "dp", None),
        P("expert", "dp", None),
    )
    shards = dense_shards if mesh.shape["expert"] <= 2 * TOPK else routed_shards
    return jax.shard_map(
        shards,
        mesh=mesh,
        in_specs=placed,
        out_specs=(P("expert", "dp", None), P("expert", "dp", None), P("expert", "dp", None)),
        check_vma=False,
    )
```

profile of v0, /device:TPU:0, one launch (start us, length us, event | category | flops | bytes accessed | tf_op | source)
XLA Modules:
  0.0 284.1 jit_solution(15623975847709586878)
XLA Ops:
  7.2 0.0 all-gather.3.cloned.1.call-start
  7.2 0.7 all-gather.3.cloned.1.call-update
  7.9 0.0 all-gather.5.cloned.1.call-start
  7.9 0.7 all-gather.5.cloned.1.call-update
  8.7 0.7 subtract_bitcast_fusion
  9.3 0.7 pad_maximum_fusion
  10.0 0.7 select_reduce_fusion
  10.7 44.2 %all_gather.10 = f32[4,4096]{1,0:T(4,128)S(1)} all-gather(f32[4,128]{1,0:T(4,128)S(1)} %select_reduce_fusion), channel_id=1, replica_groups=mesh['dp'=8,'expert'=4] {'dp','expert'}, dimensions={1}, use_global_device_ids=true | all-gather | bytes 67584 | tf_op jit(solution)/shard_map/all_gather | solution.py:130
  54.9 73.1 %all-gather.3.cloned.1.call-done = bf16[4096,2048]{1,0:T(8,128)(2,1)} async-done(((bf16[128,2048]{1,0:T(8,128)(2,1)}), bf16[4096,2048]{1,0:T(8,128)(2,1)}) %all-gather.3.cloned.1.call-update) | async-done | bytes 16777232 | tf_op jit(solution)/shard_map/all_gather | solution.py:132
  128.0 0.0 copy-start
  128.0 21.3 %fusion.4 = f32[896,4096]{1,0:T(8,128)} fusion(bf16[4096,2048]{1,0:T(8,128)(2,1)} %all-gather.3.cloned.1.call-done, bf16[1,896,2048]{2,1,0:T(8,128)(2,1)} %param.13), kind=kOutput, calls=%fused_computation.8 | convolution fusion | flops 15032385536 | bytes 35127296 | tf_op jit(solution)/shard_map/dot_general | solution.py:135
  149.3 0.0 copy-done
  149.3 23.7 %multiply_convert_fusion = bf16[896,4096]{1,0:T(8,128)(2,1)} fusion(f32[896,4096]{1,0:T(8,128)} %fusion.4, bf16[4096,2048]{1,0:T(8,128)(2,1)} %all-gather.3.cloned.1.call-done, f32[4096]{0:T(1024)S(1)} %bitcast.27, bf16[1,896,2048]{2,1,0:T(8,128)(2,1)S(1)} %copy-done), kind=kOutput, calls=%fused_computation | convolution fusion | flops 15058075648 | bytes 42483712 | tf_op jit(solution)/shard_map/dot_general | solution.py:136
  173.0 70.5 %all-gather.5.cloned.1.call-done = bf16[4096,2048]{1,0:T(8,128)(2,1)} async-done(((bf16[128,2048]{1,0:T(8,128)(2,1)}), bf16[4096,2048]{1,0:T(8,128)(2,1)}) %all-gather.5.cloned.1.call-update) | async-done | bytes 16777232 | tf_op jit(solution)/shard_map/all_gather | solution.py:133
  243.5 33.8 %multiply_add_fusion = (f32[1,896,2048]{2,1,0:T(8,128)}, f32[1,896,2048]{2,1,0:T(8,128)}, f32[1,896,2048]{2,1,0:T(8,128)}) fusion(f32[1,896,2048]{2,1,0:T(8,128)} %param.16, f32[1,896,2048]{2,1,0:T(8,128)} %param.15, f32[1,896,2048]{2,1,0:T(8,128)} %param.17, bf16[896,4096]{1,0:T(8,128)(2,1)} %multiply_convert_fusion, ...), kind=kOutput, calls=%fused_computation.6 | convolution fusion | flops 15065415680 | bytes 68157440 | tf_op jit(solution)/shard_map/dot_general | solution.py:138
  (1 shorter events, 0.0 us)
Async XLA Ops:
  7.2 120.8 %all-gather.3.cloned.1.call-start = ((), (), s32[]{:S(2)}) async-start(), calls=%async_computation | async-start | bytes 17301504 | tf_op jit(solution)/shard_map/all_gather | solution.py:132
  7.9 235.6 %all-gather.5.cloned.1.call-start = ((), (), s32[]{:S(2)}) async-start(), calls=%async_computation.1 | async-start | bytes 17301504 | tf_op jit(solution)/shard_map/all_gather | solution.py:133
  128.0 21.3 %copy-start = (bf16[1,896,2048]{2,1,0:T(8,128)(2,1)S(1)}, bf16[1,896,2048]{2,1,0:T(8,128)(2,1)}, u32[]{:S(2)}) copy-start(bf16[1,896,2048]{2,1,0:T(8,128)(2,1)} %param.14) | copy-start | bytes 11010052
Sparse Core Ops, SparseCore 0:
  10.8 117.1 all-gather.2
  130.9 112.5 all-gather.4
where the time goes:
time: 284 us
  waiting for transfers between devices  145 us (51%)
  matrix products  78.8 us (28%)
  blocking collectives  44.2 us (16%)
  between operations  14 us (5%)
    all_gather x1, waiting for transfers between devices, dense_shards(): rows = lax.all_gather(tokens, axes, axis=0, tiled=True)  73.1 us
    all_gather x1, waiting for transfers between devices, dense_shards(): grads = lax.all_gather(cotangent, axes, axis=0, tiled=True)  70.5 us
    all_gather x1, blocking collectives, dense_shards(): share = lax.all_gather(table, axes, axis=1, tiled=True)  44.2 us
    dot_general x1, matrix products, dense_shards(): gradient = jnp.dot(hidden, grads, preferred_element_type=jnp.float32)  33.8 us
    dot_general x1, matrix products, dense_shards(): lax.dot_general(up_proj[0], rows, dims, preferred_element_type=jnp.float32)  23.7 us
    dot_general x1, matrix products, dense_shards(): lax.dot_general(gate_proj[0], rows, dims, preferred_element_type=jnp.floa...  21.3 us
  transfers between devices with their start and end apart: 2, of which 2 were waited for; matrix products, arithmetic and copies ran while one was open for 17% of the time, Pallas kernels for 0%

commit v1 on v0

--- a/solution.py
+++ b/solution.py
@@ -127,7 +127,7 @@
     experts_all = lax.axis_size("expert")
     axes = ("dp", "expert")
     table = expert_shares(expert_ids, route_share, experts_all)
-    share = lax.all_gather(table, axes, axis=1, tiled=True)
+    share = jnp.concatenate(lax.all_gather(table, axes), axis=1)
     share = lax.dynamic_index_in_dim(share, lax.axis_index("expert"), 0, keepdims=True)
     rows = lax.all_gather(tokens, axes, axis=0, tiled=True)
     grads = lax.all_gather(cotangent, axes, axis=0, tiled=True)

time: 284 us -> 284 us (level)
  no operation moved by 1% of the time
where the time goes in v1:
time: 284 us
  waiting for transfers between devices  145 us (51%)
  matrix products  78.8 us (28%)
  blocking collectives  44.2 us (16%)
  between operations  14 us (5%)
    all_gather x1, waiting for transfers between devices, dense_shards(): rows = lax.all_gather(tokens, axes, axis=0, tiled=True)  73.1 us
    all_gather x1, waiting for transfers between devices, dense_shards(): grads = lax.all_gather(cotangent, axes, axis=0, tiled=True)  70.5 us
    all_gather x1, blocking collectives, dense_shards(): share = jnp.concatenate(lax.all_gather(table, axes), axis=1)  44.2 us
    dot_general x1, matrix products, dense_shards(): gradient = jnp.dot(hidden, grads, preferred_element_type=jnp.float32)  33.8 us
    dot_general x1, matrix products, dense_shards(): lax.dot_general(up_proj[0], rows, dims, preferred_element_type=jnp.float32)  23.7 us
    dot_general x1, matrix products, dense_shards(): lax.dot_general(gate_proj[0], rows, dims, preferred_element_type=jnp.floa...  21.3 us
  transfers between devices with their start and end apart: 2, of which 2 were waited for; matrix products, arithmetic and copies ran while one was open for 17% of the time, Pallas kernels for 0%

profile of v1, /device:TPU:0, one launch (start us, length us, event | category | flops | bytes accessed | tf_op | source)
XLA Modules:
  0.0 284.1 jit_solution(7384932164250804194)
XLA Ops:
  7.2 0.0 all-gather.5.cloned.1.call-start
  7.2 0.7 all-gather.5.cloned.1.call-update
  7.9 0.0 all-gather.7.cloned.1.call-start
  7.9 0.7 all-gather.7.cloned.1.call-update
  8.7 0.7 subtract_bitcast_fusion
  9.3 0.7 pad_maximum_fusion
  10.0 0.7 select_reduce_fusion
  10.7 44.2 %all-gather.1 = f32[32,4,128]{2,1,0:T(4,128)S(1)} all-gather(f32[1,4,128]{2,1,0:T(4,128)S(1)} %bitcast.33), channel_id=2, replica_groups=mesh['dp'=8,'expert'=4] {'dp','expert'}, dimensions={0}, use_global_device_ids=true | all-gather | bytes 67584 | tf_op jit(solution)/shard_map/all_gather | solution.py:130
  54.9 73.1 %all-gather.5.cloned.1.call-done = bf16[4096,2048]{1,0:T(8,128)(2,1)} async-done(((bf16[128,2048]{1,0:T(8,128)(2,1)}), bf16[4096,2048]{1,0:T(8,128)(2,1)}) %all-gather.5.cloned.1.call-update) | async-done | bytes 16777232 | tf_op jit(solution)/shard_map/all_gather | solution.py:132
  128.0 0.0 copy-start
  128.0 21.3 %fusion.4 = f32[896,4096]{1,0:T(8,128)} fusion(bf16[4096,2048]{1,0:T(8,128)(2,1)} %all-gather.5.cloned.1.call-done, bf16[1,896,2048]{2,1,0:T(8,128)(2,1)} %param.13), kind=kOutput, calls=%fused_computation.8 | convolution fusion | flops 15032385536 | bytes 35127296 | tf_op jit(solution)/shard_map/dot_general | solution.py:135
  149.3 0.0 copy-done
  149.3 23.7 %multiply_convert_fusion = bf16[896,4096]{1,0:T(8,128)(2,1)} fusion(f32[896,4096]{1,0:T(8,128)} %fusion.4, bf16[4096,2048]{1,0:T(8,128)(2,1)} %all-gather.5.cloned.1.call-done, f32[4096]{0:T(1024)S(1)} %bitcast.32, bf16[1,896,2048]{2,1,0:T(8,128)(2,1)S(1)} %copy-done), kind=kOutput, calls=%fused_computation | convolution fusion | flops 15058075648 | bytes 42483712 | tf_op jit(solution)/shard_map/dot_general | solution.py:136
  173.0 70.5 %all-gather.7.cloned.1.call-done = bf16[4096,2048]{1,0:T(8,128)(2,1)} async-done(((bf16[128,2048]{1,0:T(8,128)(2,1)}), bf16[4096,2048]{1,0:T(8,128)(2,1)}) %all-gather.7.cloned.1.call-update) | async-done | bytes 16777232 | tf_op jit(solution)/shard_map/all_gather | solution.py:133
  243.5 33.8 %multiply_add_fusion = (f32[1,896,2048]{2,1,0:T(8,128)}, f32[1,896,2048]{2,1,0:T(8,128)}, f32[1,896,2048]{2,1,0:T(8,128)}) fusion(f32[1,896,2048]{2,1,0:T(8,128)} %param.16, f32[1,896,2048]{2,1,0:T(8,128)} %param.15, f32[1,896,2048]{2,1,0:T(8,128)} %param.17, bf16[896,4096]{1,0:T(8,128)(2,1)} %multiply_convert_fusion, ...), kind=kOutput, calls=%fused_computation.6 | convolution fusion | flops 15065415680 | bytes 68157440 | tf_op jit(solution)/shard_map/dot_general | solution.py:138
  (1 shorter events, 0.0 us)
Async XLA Ops:
  7.2 120.8 %all-gather.5.cloned.1.call-start = ((), (), s32[]{:S(2)}) async-start(), calls=%async_computation | async-start | bytes 17301504 | tf_op jit(solution)/shard_map/all_gather | solution.py:132
  7.9 235.6 %all-gather.7.cloned.1.call-start = ((), (), s32[]{:S(2)}) async-start(), calls=%async_computation.1 | async-start | bytes 17301504 | tf_op jit(solution)/shard_map/all_gather | solution.py:133
  128.0 21.3 %copy-start = (bf16[1,896,2048]{2,1,0:T(8,128)(2,1)S(1)}, bf16[1,896,2048]{2,1,0:T(8,128)(2,1)}, u32[]{:S(2)}) copy-start(bf16[1,896,2048]{2,1,0:T(8,128)(2,1)} %param.14) | copy-start | bytes 11010052
Sparse Core Ops, SparseCore 0:
  10.8 117.1 all-gather.4
  130.9 112.5 all-gather.6

commit v2 on v0

--- a/solution.py
+++ b/solution.py
@@ -129,8 +129,11 @@
     table = expert_shares(expert_ids, route_share, experts_all)
     share = lax.all_gather(table, axes, axis=1, tiled=True)
     share = lax.dynamic_index_in_dim(share, lax.axis_index("expert"), 0, keepdims=True)
-    rows = lax.all_gather(tokens, axes, axis=0, tiled=True)
-    grads = lax.all_gather(cotangent, axes, axis=0, tiled=True)
+    rows, grads = jnp.split(
+        lax.all_gather(jnp.concatenate([tokens, cotangent], axis=1), axes, axis=0, tiled=True),
+        [tokens.shape[1]],
+        axis=1,
+    )
     dims = (((1,), (1,)), ((), ()))
     gate_act = lax.dot_general(gate_proj[0], rows, dims, preferred_element_type=jnp.float32)
     up_act = lax.dot_general(up_proj[0], rows, dims, preferred_element_type=jnp.float32)

time: 284 us -> 296 us (1.042)
  waiting for transfers between devices: 145 us -> 153 us
    all_gather x2 -> x1, waiting for transfers between devices: 144 us -> 153 us  [dense_shards(): lax.all_gather(jnp.concatenate([tokens, cotangent], axis=1), axes, axis=0...]
  transfers between devices with their start and end apart: 2 -> 1, of which waited for: 2 -> 1; matrix products, arithmetic and copies ran while one was open for 17% -> 1% of each run, Pallas kernels for 0% -> 0%
where the time goes in v2:
time: 296 us
  waiting for transfers between devices  153 us (52%)
  matrix products  80.2 us (27%)
  blocking collectives  44.3 us (15%)
  between operations  14 us (5%)
  other arithmetic  4.28 us (1%)
    all_gather x1, waiting for transfers between devices, dense_shards(): lax.all_gather(jnp.concatenate([tokens, cotangent], axis=1), axes, axis=0...  153 us
    all_gather x1, blocking collectives, dense_shards(): share = lax.all_gather(table, axes, axis=1, tiled=True)  44.3 us
    dot_general x1, matrix products, dense_shards(): gradient = jnp.dot(hidden, grads, preferred_element_type=jnp.float32)  31.1 us
    dot_general x1, matrix products, dense_shards(): lax.dot_general(up_proj[0], rows, dims, preferred_element_type=jnp.float32)  25.6 us
    dot_general x1, matrix products, dense_shards(): lax.dot_general(gate_proj[0], rows, dims, preferred_element_type=jnp.floa...  23.5 us
  transfers between devices with their start and end apart: 1, of which 1 were waited for; matrix products, arithmetic and copies ran while one was open for 1% of the time, Pallas kernels for 0%

profile of v2, /device:TPU:0, one launch (start us, length us, event | category | flops | bytes accessed | tf_op | source)
XLA Modules:
  0.0 295.6 jit_solution(12949898858500436917)
XLA Ops:
  7.2 0.0 all-gather.2.cloned.1.call-start
  7.2 2.3 pad_maximum_fusion
  9.5 0.0 all-gather.2.cloned.1.call-update
  9.5 0.7 subtract_bitcast_fusion
  10.2 0.7 pad_maximum_fusion.1
  10.8 0.7 select_reduce_fusion
  11.5 44.3 %all_gather.7 = f32[4,4096]{1,0:T(4,128)S(1)} all-gather(f32[4,128]{1,0:T(4,128)S(1)} %select_reduce_fusion), channel_id=1, replica_groups=mesh['dp'=8,'expert'=4] {'dp','expert'}, dimensions={1}, use_global_device_ids=true | all-gather | bytes 67584 | tf_op jit(solution)/shard_map/all_gather | solution.py:130
  55.8 152.7 %all-gather.2.cloned.1.call-done = bf16[4096,4096]{1,0:T(8,128)(2,1)} async-done(((bf16[128,4096]{1,0:T(8,128)(2,1)}), bf16[4096,4096]{1,0:T(8,128)(2,1)}) %all-gather.2.cloned.1.call-update) | async-done | bytes 33554448 | tf_op jit(solution)/shard_map/all_gather | solution.py:133
  208.5 0.0 copy-start
  208.5 23.5 %fusion.4 = f32[4096,896]{1,0:T(8,128)} fusion(bf16[4096,4096]{1,0:T(8,128)(2,1)} %all-gather.2.cloned.1.call-done, bf16[1,896,2048]{2,1,0:T(8,128)(2,1)} %param.13), kind=kOutput, calls=%fused_computation.4 | convolution fusion | flops 15032385536 | bytes 35127296 | tf_op jit(solution)/shard_map/dot_general | solution.py:138
  232.1 0.0 copy-done
  232.1 25.6 %fusion.7.clone.1.clone.5 = bf16[896,4096]{0,1:T(8,128)(2,1)} fusion(f32[4096,896]{1,0:T(8,128)} %fusion.4, bf16[4096,4096]{1,0:T(8,128)(2,1)} %all-gather.2.cloned.1.call-done, f32[4096]{0:T(1024)S(1)} %bitcast.66, bf16[1,896,2048]{2,1,0:T(8,128)(2,1)S(1)} %copy-done), kind=kOutput, calls=%fused_computation.8.clone.clone.clone.clone.clone.2 | convolution fusion | flops 15058075648 | bytes 42483712 | tf_op jit(solution)/shard_map/dot_general | solution.py:139
  257.7 31.1 %multiply_add_fusion = (f32[1,896,2048]{2,1,0:T(8,128)}, f32[1,896,2048]{2,1,0:T(8,128)}, f32[1,896,2048]{2,1,0:T(8,128)}) fusion(f32[1,896,2048]{2,1,0:T(8,128)} %param.16, f32[1,896,2048]{2,1,0:T(8,128)} %param.15, f32[1,896,2048]{2,1,0:T(8,128)} %param.17, bf16[4096,4096]{1,0:T(8,128)(2,1)} %all-gather.2.cloned.1.call-done, ...), kind=kOutput, calls=%fused_computation.19 | convolution fusion | flops 15065415680 | bytes 68157440 | tf_op jit(solution)/shard_map/dot_general | solution.py:141
  (1 shorter events, 0.0 us)
Async XLA Ops:
  7.2 201.4 %all-gather.2.cloned.1.call-start = ((), (), s32[]{:S(2)}) async-start(), calls=%async_computation | async-start | bytes 34603008 | tf_op jit(solution)/shard_map/all_gather | solution.py:133
  208.5 23.5 %copy-start = (bf16[1,896,2048]{2,1,0:T(8,128)(2,1)S(1)}, bf16[1,896,2048]{2,1,0:T(8,128)(2,1)}, u32[]{:S(2)}) copy-start(bf16[1,896,2048]{2,1,0:T(8,128)(2,1)} %param.14) | copy-start | bytes 11010052
Sparse Core Ops, SparseCore 0:
  11.4 197.0 all-gather.1
